TPU v7x, 32 devices: a whole 2x2x4 slice. The times are simulated.
32 devices in a mesh: dp: 2 (over x), expert: 16 (over z, y, core).
Axes of the slice: x: 2, y: 2, z: 4, core: 2. Of those that a mesh axis runs over, the one named last changes fastest.
Arguments:
- tokens_in: bfloat16 [4096, 2880], P(('dp', 'expert')), may hold values from -6 to 6
- grad_out: bfloat16 [4096, 2880], P(('dp', 'expert')), may hold values from -6 to 6
- expert_ids: int32 [4096, 4], P(('dp', 'expert')), may hold values from 0 to 15, all different within a row; in each aligned block of 128 rows (0 to 127, 128 to 255, ...) at most 40 rows name the same one
- combine_weights: float32 [4096, 4], P(('dp', 'expert')), may hold values from 0.1 to 1
- up_weight: bfloat16 [16, 2880, 1440], P('expert'), may hold values from -0.109375 to 0.109375
- down_weight: bfloat16 [16, 1440, 2880], P('expert'), may hold values from -0.15625 to 0.15625
Outputs:
- grad_input: bfloat16 [4096, 2880], P(('dp', 'expert'))
- grad_up: bfloat16 [16, 2880, 1440], P('expert', 'dp')
- grad_down: bfloat16 [16, 1440, 2880], P('expert', 'dp')
Inputs may be any that keep to these rules, and one draw needn't show every extreme that they name: `expert_ids`: each row names 4 different experts; in the rows of one device no expert is named by more than 40 rows, a bound that some block reaches.
All inputs are finite; a program needn't handle non-finite values.
Results may differ from a plain program's by a relative error of at most 0.0064.
Values may be sent and summed in bfloat16 or wider, within the bound.
A program may use at most 192 MiB of HBM per device.

v0:
```python
import jax
import jax.numpy as jnp
from jax import lax
from jax.sharding import PartitionSpec as P


def silu_parts(preact):
    logistic = jax.nn.sigmoid(preact)
    return (preact * logistic, logistic * (1.0 + preact * (1.0 - logistic)))


def contract_rows(left, right):
    return lax.dot_general(
        left, right, (((0,), (0,)), ((), ())), preferred_element_type=jnp.float32
    )


def contract_cols(left, right):
    return lax.dot_general(
        left, right, (((1,), (1,)), ((), ())), preferred_element_type=jnp.float32
    )


def local(tokens_in, grad_out, expert_ids, combine_weights, up_weight, down_weight):
    token_count, model_width = tokens_in.shape
    top_count = expert_ids.shape[1]
    expert_group = lax.axis_size("expert")
    experts_all = expert_group * up_weight.shape[0]
    capacity = 5 * token_count * top_count // (4 * experts_all)
    routed = token_count * top_count
    flat_ids = expert_ids.reshape(-1)
    one_hot = (flat_ids[:, None] == jnp.arange(experts_all, dtype=jnp.int32)[None, :]).astype(
        jnp.int32
    )
    slot_rank = jnp.sum((jnp.cumsum(one_hot, axis=0) - one_hot) * one_hot, axis=1)
    position = flat_ids * capacity + slot_rank
    slot_table = (
        jnp.full((experts_all * capacity,), routed, jnp.int32)
        .at[position]
        .set(jnp.arange(routed, dtype=jnp.int32))
    )
    source_token = slot_table // top_count
    padded_x = jnp.concatenate([tokens_in, jnp.zeros((1, model_width), tokens_in.dtype)], axis=0)
    padded_dy = jnp.concatenate([grad_out, jnp.zeros((1, model_width), grad_out.dtype)], axis=0)
    padded_weight = jnp.concatenate(
        [combine_weights.reshape(-1), jnp.zeros((1,), jnp.float32)], axis=0
    )
    send_x = padded_x[source_token].reshape(experts_all, capacity, model_width)
    send_grad = (
        padded_weight[slot_table][:, None] * padded_dy[source_token].astype(jnp.float32)
    ).astype(jnp.bfloat16)
    send_grad = send_grad.reshape(experts_all, capacity, model_width)
    w_up = up_weight[0]
    w_down = down_weight[0]
    hidden_width = w_up.shape[1]
    slot_x = lax.all_to_all(send_x, "expert", split_axis=0, concat_axis=0, tiled=True)
    slot_grad = lax.all_to_all(send_grad, "expert", split_axis=0, concat_axis=0, tiled=True)
    sources = slot_x.shape[0]
    slot_count = slot_x.shape[1]
    rows_x = slot_x.reshape(-1, model_width)
    rows_grad = slot_grad.reshape(-1, model_width)
    preact = jnp.dot(rows_x, w_up, preferred_element_type=jnp.float32)
    activated, slope = silu_parts(preact)
    activated = activated.astype(jnp.bfloat16)
    grad_act = contract_cols(rows_grad, w_down)
    grad_pre = (grad_act * slope).astype(jnp.bfloat16)
    grad_rows = (
        contract_cols(grad_pre, w_up).astype(jnp.bfloat16).reshape(sources, slot_count, model_width)
    )
    returned = lax.all_to_all(grad_rows, "expert", split_axis=0, concat_axis=0, tiled=True)
    returned, activated, grad_pre, slot_x, slot_grad = (
        returned,
        activated.reshape(sources, slot_count, hidden_width),
        grad_pre.reshape(sources, slot_count, hidden_width),
        slot_x,
        slot_grad,
    )
    picked = returned.reshape(-1, model_width)[position].reshape(
        token_count, top_count, model_width
    )
    grad_input = jnp.sum(picked.astype(jnp.float32), axis=1).astype(jnp.bfloat16)
    rows_x = slot_x.reshape(-1, model_width)
    rows_grad = slot_grad.reshape(-1, model_width)
    activated = activated.reshape(-1, hidden_width)
    grad_pre = grad_pre.reshape(-1, hidden_width)
    column_x, column_act = (
        lax.all_to_all(rows_x, "dp", split_axis=1, concat_axis=0, tiled=True),
        lax.all_to_all(activated, "dp", split_axis=1, concat_axis=0, tiled=True),
    )
    every_pre, every_grad = (
        lax.all_gather(grad_pre, "dp", axis=0, tiled=True),
        lax.all_gather(rows_grad, "dp", axis=0, tiled=True),
    )
    grad_up = contract_rows(column_x, every_pre)
    grad_down = contract_rows(column_act, every_grad)
    return (grad_input, grad_up.astype(jnp.bfloat16)[None], grad_down.astype(jnp.bfloat16)[None])


def solution(mesh):
    return jax.shard_map(
        local,
        mesh=mesh,
        in_specs=(
            P(("dp", "expert"), None),
            P(("dp", "expert"), None),
            P(("dp", "expert"), None),
            P(("dp", "expert"), None),
            P("expert", None, None),
            P("expert", None, None),
        ),
        out_specs=(P(("dp", "expert"), None), P("expert", "dp", None), P("expert", "dp", None)),
        check_vma=False,
    )
```

profile of v0, /device:TPU:13, one launch (start us, length us, event | category | flops | bytes accessed | tf_op | source)
XLA Modules:
  0.0 450.4 jit_solution(9716306329812770657)
XLA Ops:
  7.2 0.7 broadcast_multiply_fusion
  7.8 0.8 copy.24
  8.6 0.1 eq.25
  8.7 0.1 eq.29
  8.9 1.5 copy.28
  10.3 0.1 copy.23
  10.4 0.1 mul.44
  10.5 1.2 reduce-window.6
  11.7 0.2 slice_reduce_fusion
  12.0 0.1 fusion.20
  12.1 2.4 scatter_custom_fusion
  14.6 0.1 concatenate.11
  14.6 4.6 %gather_fusion.2 = bf16[640,2880]{1,0:T(8,128)(2,1)} fusion(bf16[129,2880]{1,0:T(8,128)(2,1)S(1)} %concatenate.11, s32[1024]{0:T(1024)S(1)} %get-tuple-element.10), kind=kCustom, calls=%fused_computation.2 | custom fusion | bytes 7375360 | tf_op jit(solution)/shard_map/gather | solution.py:48
  19.2 0.0 copy-start
  19.2 6.7 %all-to-all-start.1 = ((bf16[16,40,2880]{2,1,0:T(8,128)(2,1)}), bf16[16,40,2880]{2,1,0:T(8,128)(2,1)}, u32[]{:S(2)}, u32[]{:S(2)}) async-start(bf16[16,40,2880]{2,1,0:T(8,128)(2,1)} %bitcast.62), calls=%async_computation.1 | async-start | bytes 7536640 | tf_op jit(solution)/shard_map/all_to_all | solution.py:56
  25.8 0.0 copy-done
  25.8 0.3 copy.27
  26.2 0.1 concatenate.10
  26.3 0.0 copy-start.1
  26.3 4.6 %gather_fusion.1 = bf16[640,2880]{1,0:T(8,128)(2,1)} fusion(bf16[129,2880]{1,0:T(8,128)(2,1)S(1)} %concatenate.10, s32[1024]{0:T(1024)S(1)} %get-tuple-element.10), kind=kCustom, calls=%fused_computation.1 | custom fusion | bytes 7375360 | tf_op jit(solution)/shard_map/gather | solution.py:50
  30.8 0.0 copy-done.1
  30.8 0.1 copy.22
  30.9 0.1 reshape.92
  31.1 2.8 gather_fusion
  33.9 0.1 mul.46
  33.9 5.0 %fusion.6 = bf16[16,40,2880]{2,1,0:T(8,128)(2,1)} fusion(bf16[16,40,2880]{2,1,0:T(8,128)(2,1)} %bitcast.63, f32[16,40]{1,0:T(8,128)S(1)} %mul.46), kind=kLoop, calls=%fused_computation.13 | loop fusion | flops 5529600 | bytes 7375360 | tf_op jit(solution)/shard_map/convert_element_type | solution.py:51
  38.9 70.2 %all-to-all-done.1 = bf16[16,40,2880]{2,1,0:T(8,128)(2,1)} async-done(((bf16[16,40,2880]{2,1,0:T(8,128)(2,1)}), bf16[16,40,2880]{2,1,0:T(8,128)(2,1)}, u32[]{:S(2)}, u32[]{:S(2)}) %all-to-all-start.1) | async-done | bytes 3686432 | tf_op jit(solution)/shard_map/all_to_all | solution.py:56
  109.2 4.8 %all-to-all-start = ((bf16[16,40,2880]{2,1,0:T(8,128)(2,1)}), bf16[16,40,2880]{2,1,0:T(8,128)(2,1)}, u32[]{:S(2)}, u32[]{:S(2)}) async-start(bf16[16,40,2880]{2,1,0:T(8,128)(2,1)} %fusion.6), calls=%async_computation | async-start | bytes 7536640 | tf_op jit(solution)/shard_map/all_to_all | solution.py:57
  114.0 0.0 all-gather.3.cloned.1.call-start
  114.0 12.3 %multiply_convert_fusion = (bf16[640,1440]{0,1:T(8,128)(2,1)}, f32[640,1440]{0,1:T(8,128)}) fusion(bf16[640,2880]{1,0:T(8,128)(2,1)} %bitcast.7, bf16[1,2880,1440]{1,2,0:T(8,128)(2,1)} %param.10), kind=kOutput, calls=%fused_computation.19 | convolution fusion | flops 5313024000 | bytes 17510400 | tf_op jit(solution)/shard_map/dot_general | solution.py:62
  126.3 71.0 %all-to-all-done = bf16[16,40,2880]{2,1,0:T(8,128)(2,1)} async-done(((bf16[16,40,2880]{2,1,0:T(8,128)(2,1)}), bf16[16,40,2880]{2,1,0:T(8,128)(2,1)}, u32[]{:S(2)}, u32[]{:S(2)}) %all-to-all-start) | async-done | bytes 3686432 | tf_op jit(solution)/shard_map/all_to_all | solution.py:57
  197.3 12.4 %fusion.15 = bf16[640,1440]{0,1:T(8,128)(2,1)} fusion(f32[640,1440]{0,1:T(8,128)} %get-tuple-element.9, bf16[640,2880]{1,0:T(8,128)(2,1)} %bitcast.4, bf16[1,1440,2880]{2,1,0:T(8,128)(2,1)} %param.11), kind=kOutput, calls=%fused_computation.21 | convolution fusion | flops 5316710400 | bytes 17510400 | tf_op jit(solution)/shard_map/dot_general | solution.py:19
  209.7 0.0 all-gather.3.cloned.1.call-update
  209.7 3.9 all-to-all-start.4
  213.6 11.5 %all_to_all.40 = bf16[640,2,1440]{2,1,0:T(2,128)(2,1)} reshape(bf16[16,40,2880]{2,1,0:T(8,128)(2,1)} %all-to-all-done.1) | data formatting | bytes 7372800 | tf_op jit(solution)/shard_map/all_to_all | solution.py:87
  225.1 10.6 %copy.30 = bf16[640,2,1440]{0,2,1:T(8,128)(2,1)} copy(bf16[640,2,1440]{2,1,0:T(2,128)(2,1)} %all_to_all.40) | data formatting | bytes 7372800 | tf_op jit(solution)/shard_map/all_to_all | solution.py:87
  235.7 14.6 %all-to-all-done.4 = bf16[640,2,720]{0,2,1:T(8,128)(2,1)S(1)} async-done(((bf16[640,2,720]{0,2,1:T(8,128)(2,1)}), bf16[640,2,720]{0,2,1:T(8,128)(2,1)S(1)}, u32[]{:S(2)}, u32[]{:S(2)}) %all-to-all-start.4) | async-done | bytes 1843232 | tf_op jit(solution)/shard_map/all_to_all | solution.py:88
  250.3 5.4 %all-to-all-start.3 = ((bf16[640,2,1440]{0,2,1:T(8,128)(2,1)}), bf16[640,2,1440]{0,2,1:T(8,128)(2,1)}, u32[]{:S(2)}, u32[]{:S(2)}) async-start(bf16[640,2,1440]{0,2,1:T(8,128)(2,1)} %copy.30), calls=%async_computation.3 | async-start | bytes 7372800 | tf_op jit(solution)/shard_map/all_to_all | solution.py:87
  255.8 0.0 all-gather.5.cloned.1.call-start
  255.8 0.7 all-gather.5.cloned.1.call-update
  256.5 11.8 %fusion.8 = bf16[640,2880]{0,1:T(8,128)(2,1)} fusion(bf16[640,1440]{0,1:T(8,128)(2,1)} %fusion.15, bf16[1,2880,1440]{1,2,0:T(8,128)(2,1)} %param.10), kind=kOutput, calls=%fused_computation.16 | convolution fusion | flops 5310259200 | bytes 13824000 | tf_op jit(solution)/shard_map/dot_general | solution.py:19
  268.4 6.2 %copy.29 = bf16[640,2880]{1,0:T(8,128)(2,1)} copy(bf16[640,2880]{0,1:T(8,128)(2,1)} %fusion.8) | data formatting | bytes 7372800 | tf_op jit(solution)/shard_map/convert_element_type | solution.py:68
  274.5 47.1 %all-to-all-done.3 = bf16[640,2,1440]{0,2,1:T(8,128)(2,1)} async-done(((bf16[640,2,1440]{0,2,1:T(8,128)(2,1)}), bf16[640,2,1440]{0,2,1:T(8,128)(2,1)}, u32[]{:S(2)}, u32[]{:S(2)}) %all-to-all-start.3) | async-done | bytes 3686432 | tf_op jit(solution)/shard_map/all_to_all | solution.py:87
  321.7 6.6 %all-to-all-start.2 = ((bf16[16,40,2880]{2,1,0:T(8,128)(2,1)}), bf16[16,40,2880]{2,1,0:T(8,128)(2,1)}, u32[]{:S(2)}, u32[]{:S(2)}) async-start(bf16[16,40,2880]{2,1,0:T(8,128)(2,1)} %bitcast.64), calls=%async_computation.2 | async-start | bytes 7536640 | tf_op jit(solution)/shard_map/all_to_all | solution.py:70
  328.3 1.4 copy.36
  329.7 4.2 copy.35
  333.9 0.0 all-gather.3.cloned.1.call-done
  333.9 10.1 %fusion.7 = bf16[1,1440,1440]{2,1,0:T(8,128)(2,1)} fusion(bf16[1280,1440]{0,1:T(8,128)(2,1)} %bitcast.66, bf16[1280,1440]{0,1:T(8,128)(2,1)} %all-gather.3.cloned.1.call-done), kind=kOutput, calls=%fused_computation.14 | convolution fusion | flops 5310489600 | bytes 11520000 | tf_op jit(solution)/shard_map/dot_general | solution.py:13
  344.0 67.6 %all-to-all-done.2 = bf16[16,40,2880]{2,1,0:T(8,128)(2,1)} async-done(((bf16[16,40,2880]{2,1,0:T(8,128)(2,1)}), bf16[16,40,2880]{2,1,0:T(8,128)(2,1)}, u32[]{:S(2)}, u32[]{:S(2)}) %all-to-all-start.2) | async-done | bytes 3686432 | tf_op jit(solution)/shard_map/all_to_all | solution.py:70
  411.6 9.3 %gather_fusion.3 = bf16[512,2880]{1,0:T(8,128)(2,1)} fusion(bf16[640,2880]{1,0:T(8,128)(2,1)} %bitcast.10, s32[1024]{0:T(1024)S(1)} %pad_clamp_fusion), kind=kCustom, calls=%fused_computation.3 | custom fusion | bytes 5900288 | tf_op jit(solution)/shard_map/gather | solution.py:78
  420.9 4.7 %reshape.99 = bf16[128,4,2880]{2,1,0:T(4,128)(2,1)S(1)} reshape(bf16[512,2880]{1,0:T(8,128)(2,1)} %gather_fusion.3) | data formatting | bytes 5898240 | tf_op jit(solution)/shard_map/reshape | solution.py:78
  425.5 4.9 %reduce_sum.25 = bf16[128,2880]{1,0:T(8,128)(2,1)} reduce(bf16[128,4,2880]{2,1,0:T(4,128)(2,1)S(1)} %reshape.99, bf16[]{:T(256)} %constant.34.clone.1), dimensions={1}, to_apply=%region_4.5 | reduce | flops 1105920 | bytes 3686402 | tf_op jit(solution)/shard_map/reduce_sum | solution.py:81
  430.5 2.3 copy.33
  432.7 0.0 all-gather.5.cloned.1.call-done
  432.7 10.8 %fusion.11 = bf16[1,720,2880]{2,1,0:T(8,128)(2,1)} fusion(bf16[1280,720]{0,1:T(8,128)(2,1)} %bitcast.67, bf16[1280,2880]{1,0:T(8,128)(2,1)} %all-gather.5.cloned.1.call-done), kind=kOutput, calls=%fused_computation.17 | convolution fusion | flops 5310489600 | bytes 13363200 | tf_op jit(solution)/shard_map/dot_general | solution.py:13
  (9 shorter events, 0.1 us)
Async XLA Ops:
  19.2 6.7 %copy-start = (bf16[128,2880]{0,1:T(8,128)(2,1)S(1)}, bf16[128,2880]{0,1:T(8,128)(2,1)}, u32[]{:S(2)}) copy-start(bf16[128,2880]{0,1:T(8,128)(2,1)} %param.7) | copy-start | bytes 2211844
  19.2 90.0 %all-to-all-start.1 = ((bf16[16,40,2880]{2,1,0:T(8,128)(2,1)}), bf16[16,40,2880]{2,1,0:T(8,128)(2,1)}, u32[]{:S(2)}, u32[]{:S(2)}) async-start(bf16[16,40,2880]{2,1,0:T(8,128)(2,1)} %bitcast.62), calls=%async_computation.1 | async-start | bytes 7536640 | tf_op jit(solution)/shard_map/all_to_all | solution.py:56
  26.3 4.6 %copy-start.1 = (f32[128,4]{0,1:T(4,128)S(1)}, f32[128,4]{0,1:T(4,128)}, u32[]{:S(2)}) copy-start(f32[128,4]{0,1:T(4,128)} %param.9) | copy-start | bytes 6148
  109.2 88.1 %all-to-all-start = ((bf16[16,40,2880]{2,1,0:T(8,128)(2,1)}), bf16[16,40,2880]{2,1,0:T(8,128)(2,1)}, u32[]{:S(2)}, u32[]{:S(2)}) async-start(bf16[16,40,2880]{2,1,0:T(8,128)(2,1)} %fusion.6), calls=%async_computation | async-start | bytes 7536640 | tf_op jit(solution)/shard_map/all_to_all | solution.py:57
  114.0 220.0 %all-gather.3.cloned.1.call-start = ((), (), s32[]{:S(2)}) async-start(), calls=%async_computation.5 | async-start | bytes 5529600 | tf_op jit(solution)/shard_map/all_gather | solution.py:91
  209.7 40.6 %all-to-all-start.4 = ((bf16[640,2,720]{0,2,1:T(8,128)(2,1)}), bf16[640,2,720]{0,2,1:T(8,128)(2,1)S(1)}, u32[]{:S(2)}, u32[]{:S(2)}) async-start(bf16[640,2,720]{0,2,1:T(8,128)(2,1)} %bitcast.68), calls=%async_computation.4 | async-start | bytes 3686400 | tf_op jit(solution)/shard_map/all_to_all | solution.py:88
  250.3 71.3 %all-to-all-start.3 = ((bf16[640,2,1440]{0,2,1:T(8,128)(2,1)}), bf16[640,2,1440]{0,2,1:T(8,128)(2,1)}, u32[]{:S(2)}, u32[]{:S(2)}) async-start(bf16[640,2,1440]{0,2,1:T(8,128)(2,1)} %copy.30), calls=%async_computation.3 | async-start | bytes 7372800 | tf_op jit(solution)/shard_map/all_to_all | solution.py:87
  255.8 177.0 %all-gather.5.cloned.1.call-start = ((), (), s32[]{:S(2)}) async-start(), calls=%async_computation.6 | async-start | bytes 11304960 | tf_op jit(solution)/shard_map/all_gather | solution.py:92
  321.7 89.9 %all-to-all-start.2 = ((bf16[16,40,2880]{2,1,0:T(8,128)(2,1)}), bf16[16,40,2880]{2,1,0:T(8,128)(2,1)}, u32[]{:S(2)}, u32[]{:S(2)}) async-start(bf16[16,40,2880]{2,1,0:T(8,128)(2,1)} %bitcast.64), calls=%async_computation.2 | async-start | bytes 7536640 | tf_op jit(solution)/shard_map/all_to_all | solution.py:70
Sparse Core Ops, SparseCore 0:
  209.8 81.7 all-gather.2
  293.2 102.6 all-gather.4
where the time goes:
time: 452 us; the launch traced here: 450 us
  waiting for transfers between devices  271 us (60%)
  local copies, waits for them, and re-layouts  68.1 us (15%)
  matrix products  57.5 us (13%)
  starting transfers between devices  27.4 us (6%)
  between operations  14.2 us (3%)
  other arithmetic  12 us (3%)
    all_to_all x1, waiting for transfers between devices, local(): lax.all_to_all(send_grad, 'expert', split_axis=0, concat_axis=0, tiled=True)  71 us
    all_to_all x1, waiting for transfers between devices, local(): lax.all_to_all(send_x, 'expert', split_axis=0, concat_axis=0, tiled=True)  70.2 us
    all_to_all x1, waiting for transfers between devices, local(): lax.all_to_all(grad_rows, 'expert', split_axis=0, concat_axis=0, tiled=True)  67.6 us
    all_to_all x1, waiting for transfers between devices, local(): lax.all_to_all(rows_x, 'dp', split_axis=1, concat_axis=0, tiled=True)  47.1 us
    all_to_all x3, local copies, waits for them, and re-layouts, local(): lax.all_to_all(rows_x, 'dp', split_axis=1, concat_axis=0, tiled=True)  26.3 us
    dot_general x2, matrix products, contract_cols(): lax.dot_general(left, right, (((1,), (1,)), ((), ())), preferred_element_...  24.2 us
    dot_general x2, matrix products, contract_rows(): lax.dot_general(left, right, (((0,), (0,)), ((), ())), preferred_element_...  20.9 us
    all_to_all x1, waiting for transfers between devices, local(): lax.all_to_all(activated, 'dp', split_axis=1, concat_axis=0, tiled=True)  14.6 us
  transfers between devices with their start and end apart: 7, of which 5 were waited for; matrix products, arithmetic and copies ran while one was open for 20% of the time, Pallas kernels for 0%

commit v1 on v0

v1 whole, which is shorter than its diff:
```python
import jax
import jax.numpy as jnp
from jax import lax
from jax.sharding import PartitionSpec as P


def silu_parts(preact):
    logistic = jax.nn.sigmoid(preact)
    return (preact * logistic, logistic * (1.0 + preact * (1.0 - logistic)))


def contract_rows(left, right):
    return lax.dot_general(
        left, right, (((0,), (0,)), ((), ())), preferred_element_type=jnp.float32
    )


def contract_cols(left, right):
    return lax.dot_general(
        left, right, (((1,), (1,)), ((), ())), preferred_element_type=jnp.float32
    )


def other_replica(value):
    pairs = lax.axis_size("dp")
    return lax.ppermute(value, "dp", [(i, (i + 1) % pairs) for i in range(pairs)])


def slots_of(expert_ids, combine_weights, experts_all, capacity):
    token_count, top_count = expert_ids.shape
    hits = expert_ids[:, :, None] == jnp.arange(experts_all, dtype=jnp.int32)[None, None, :]
    chosen = jnp.any(hits, axis=1).astype(jnp.bfloat16)
    token_index = jnp.arange(token_count, dtype=jnp.int32)
    earlier = (token_index[None, :] < token_index[:, None]).astype(jnp.bfloat16)
    rank = jnp.dot(earlier, chosen, preferred_element_type=jnp.float32).astype(jnp.int32)
    slot_rank = jnp.sum(jnp.where(hits, rank[:, None, :], 0), axis=2)
    position = expert_ids * capacity + slot_rank
    slot = jnp.arange(experts_all * capacity, dtype=jnp.int32)
    taken = jnp.zeros((token_count, experts_all * capacity), jnp.float32)
    weight = taken
    for k in range(top_count):
        match = position[:, k][:, None] == slot[None, :]
        taken = jnp.where(match, 1.0, taken)
        weight = jnp.where(match, combine_weights[:, k][:, None], weight)
    return taken.astype(jnp.bfloat16), jnp.sum(weight, axis=0)


def local(tokens_in, grad_out, expert_ids, combine_weights, up_weight, down_weight):
    token_count, _ = tokens_in.shape
    top_count = expert_ids.shape[1]
    experts_all = lax.axis_size("expert") * up_weight.shape[0]
    capacity = 5 * token_count * top_count // (4 * experts_all)
    place, slot_weight = slots_of(expert_ids, combine_weights, experts_all, capacity)
    w_up = up_weight[0]
    w_down = down_weight[0]
    replica = lax.axis_index("dp")

    def halves(value):
        half = value.shape[1] // 2
        low, high = value[:, :half], value[:, half:]
        first = replica == 0
        return jnp.where(first, low, high), jnp.where(first, high, low)

    def to_experts(rows):
        return lax.all_to_all(rows, "expert", split_axis=0, concat_axis=0, tiled=True)

    send_grad = (contract_rows(place, grad_out) * slot_weight[:, None]).astype(jnp.bfloat16)
    send_x = contract_rows(place, tokens_in).astype(jnp.bfloat16)
    rows_grad = to_experts(send_grad)
    other_grad = other_replica(rows_grad)
    rows_x = to_experts(send_x)
    grad_act = lax.optimization_barrier(contract_cols(rows_grad, w_down))
    keep_x, give_x = halves(rows_x)
    other_x = other_replica(give_x)
    preact = jnp.dot(rows_x, w_up, preferred_element_type=jnp.float32)
    activated, slope = silu_parts(preact)
    activated = activated.astype(jnp.bfloat16)
    grad_pre = (grad_act * slope).astype(jnp.bfloat16)
    keep_act, give_act = halves(activated)
    other_act = other_replica(give_act)
    other_pre = other_replica(grad_pre)
    grad_rows = contract_cols(grad_pre, w_up).astype(jnp.bfloat16)
    returned = to_experts(grad_rows)
    grad_down = contract_rows(keep_act, rows_grad) + contract_rows(other_act, other_grad)
    grad_up = contract_rows(keep_x, grad_pre) + contract_rows(other_x, other_pre)
    grad_input = jnp.dot(place, returned, preferred_element_type=jnp.float32).astype(jnp.bfloat16)
    return (grad_input, grad_up.astype(jnp.bfloat16)[None], grad_down.astype(jnp.bfloat16)[None])


def solution(mesh):
    return jax.shard_map(
        local,
        mesh=mesh,
        in_specs=(
            P(("dp", "expert"), None),
            P(("dp", "expert"), None),
            P(("dp", "expert"), None),
            P(("dp", "expert"), None),
            P("expert", None, None),
            P("expert", None, None),
        ),
        out_specs=(P(("dp", "expert"), None), P("expert", "dp", None), P("expert", "dp", None)),
        check_vma=False,
    )
```

time: 452 us -> 428 us (0.947)
  local copies, waits for them, and re-layouts: 68.1 us -> 27.7 us
  waiting for transfers between devices: 271 us -> 296 us
  matrix products: 57.5 us -> 75 us
  between operations: 14.2 us -> 0.71 us
  starting transfers between devices: 27.4 us -> 19.2 us
  other arithmetic: 12 us -> 6.69 us
    ppermute x0 -> x4, waiting for transfers between devices: none -> 150 us  [other_replica(): lax.ppermute(value, 'dp', [(i, (i + 1) % pairs) for i in range(pairs)])]
    all_to_all x5 -> x3, waiting for transfers between devices: 271 us -> 146 us  [to_experts(): lax.all_to_all(rows, 'expert', split_axis=0, concat_axis=0, tiled=True)]
    all_to_all x4 -> x1, local copies, waits for them, and re-layouts: 27.7 us -> 6.08 us  [to_experts(): lax.all_to_all(rows, 'expert', split_axis=0, concat_axis=0, tiled=True)]
    gather x4 -> x0, local copies, waits for them, and re-layouts: 21.2 us -> none  [the longest x1 9.28 us: local(): returned.reshape(-1, model_width)[position]]
    dot_general x2 -> x6, matrix products: 20.9 us -> 33.6 us  [contract_rows(): lax.dot_general(left, right, (((0,), (0,)), ((), ())), preferred_element_...]
    convert_element_type x1 -> x3, local copies, waits for them, and re-layouts: 6.16 us -> 18.5 us  [the longest x1 6.16 us: local(): (contract_rows(place, grad_out) * slot_weight[:, None]).astype(jnp.bfloat16)]
    all_to_all x5 -> x3, starting transfers between devices: 27.4 us -> 16.2 us  [to_experts(): lax.all_to_all(rows, 'expert', split_axis=0, concat_axis=0, tiled=True)]
    convert_element_type x2 -> x0, other arithmetic: 5 us -> none  [the longest x1 4.99 us: local(): send_grad = (padded_weight[slot_table][:, None] * padded_dy[source_token]...]
  transfers between devices with their start and end apart: 7 -> 7, of which waited for: 5 -> 5; matrix products, arithmetic and copies ran while one was open for 20% -> 14% of each run, Pallas kernels for 0% -> 0%
where the time goes in v1:
time: 428 us; the launch traced here: 425 us
  waiting for transfers between devices  296 us (69%)
  matrix products  75 us (18%)
  local copies, waits for them, and re-layouts  27.7 us (6%)
  starting transfers between devices  19.2 us (4%)
  other arithmetic  6.69 us (2%)
    ppermute x4, waiting for transfers between devices, other_replica(): lax.ppermute(value, 'dp', [(i, (i + 1) % pairs) for i in range(pairs)])  150 us
    all_to_all x3, waiting for transfers between devices, to_experts(): lax.all_to_all(rows, 'expert', split_axis=0, concat_axis=0, tiled=True)  146 us
    dot_general x6, matrix products, contract_rows(): lax.dot_general(left, right, (((0,), (0,)), ((), ())), preferred_element_...  33.6 us
    dot_general x2, matrix products, contract_cols(): lax.dot_general(left, right, (((1,), (1,)), ((), ())), preferred_element_...  23.7 us
    all_to_all x3, starting transfers between devices, to_experts(): lax.all_to_all(rows, 'expert', split_axis=0, concat_axis=0, tiled=True)  16.2 us
    dot_general x1, matrix products, local(): preact = jnp.dot(rows_x, w_up, preferred_element_type=jnp.float32)  13.1 us
  transfers between devices with their start and end apart: 7, of which 5 were waited for; matrix products, arithmetic and copies ran while one was open for 14% of the time, Pallas kernels for 0%

profile of v1, /device:TPU:13, one launch (start us, length us, event | category | flops | bytes accessed | tf_op | source)
XLA Modules:
  0.0 425.0 jit_solution(10402291755773165877)
XLA Ops:
  0.6 0.0 copy-start
  0.6 0.8 fusion.22
  1.4 0.1 convolution_convert_fusion.2
  1.6 0.7 select_reduce_fusion.1
  2.3 0.7 multiply_add_fusion
  3.0 0.8 slice_bitcast_fusion.3
  3.8 0.2 select_reduce_fusion
  4.0 0.0 copy-done
  4.0 3.1 multiply_convert_fusion
  7.1 6.2 %copy.23 = bf16[640,2880]{1,0:T(8,128)(2,1)} copy(bf16[640,2880]{0,1:T(8,128)(2,1)} %multiply_convert_fusion) | data formatting | bytes 7372800 | tf_op jit(solution)/shard_map/convert_element_type | solution.py:67
  13.3 0.0 copy-start.2
  13.3 6.7 %all-to-all-start = ((bf16[16,40,2880]{2,1,0:T(8,128)(2,1)}), bf16[16,40,2880]{2,1,0:T(8,128)(2,1)}, u32[]{:S(2)}, u32[]{:S(2)}) async-start(bf16[16,40,2880]{2,1,0:T(8,128)(2,1)} %bitcast.53), calls=%async_computation | async-start | bytes 7536640 | tf_op jit(solution)/shard_map/all_to_all | solution.py:65
  19.9 0.0 copy-done.2
  19.9 3.1 convolution_convert_fusion
  23.1 6.2 %copy.24 = bf16[640,2880]{1,0:T(8,128)(2,1)} copy(bf16[640,2880]{0,1:T(8,128)(2,1)} %convolution_convert_fusion) | data formatting | bytes 7372800 | tf_op jit(solution)/shard_map/convert_element_type | solution.py:68
  29.2 74.1 %all-to-all-done = bf16[16,40,2880]{2,1,0:T(8,128)(2,1)} async-done(((bf16[16,40,2880]{2,1,0:T(8,128)(2,1)}), bf16[16,40,2880]{2,1,0:T(8,128)(2,1)}, u32[]{:S(2)}, u32[]{:S(2)}) %all-to-all-start) | async-done | bytes 3686432 | tf_op jit(solution)/shard_map/all_to_all | solution.py:65
  103.3 4.8 %all-to-all-start.1 = ((bf16[16,40,2880]{2,1,0:T(8,128)(2,1)}), bf16[16,40,2880]{2,1,0:T(8,128)(2,1)}, u32[]{:S(2)}, u32[]{:S(2)}) async-start(bf16[16,40,2880]{2,1,0:T(8,128)(2,1)} %bitcast.52), calls=%async_computation.1 | async-start | bytes 7536640 | tf_op jit(solution)/shard_map/all_to_all | solution.py:65
  108.1 11.8 %fusion.4 = f32[640,1440]{0,1:T(8,128)} fusion(bf16[640,2880]{1,0:T(8,128)(2,1)} %bitcast.9, bf16[1,1440,2880]{2,1,0:T(8,128)(2,1)} %param.11), kind=kOutput, calls=%fused_computation.5 | convolution fusion | flops 5308416000 | bytes 15667200 | tf_op jit(solution)/shard_map/dot_general | solution.py:19
  119.9 71.5 %all-to-all-done.1 = bf16[16,40,2880]{2,1,0:T(8,128)(2,1)} async-done(((bf16[16,40,2880]{2,1,0:T(8,128)(2,1)}), bf16[16,40,2880]{2,1,0:T(8,128)(2,1)}, u32[]{:S(2)}, u32[]{:S(2)}) %all-to-all-start.1) | async-done | bytes 3686432 | tf_op jit(solution)/shard_map/all_to_all | solution.py:65
  191.4 13.1 %multiply_convert_fusion.1 = (bf16[640,1440]{0,1:T(8,128)(2,1)}, bf16[640,1440]{0,1:T(8,128)(2,1)}) fusion(f32[640,1440]{0,1:T(8,128)} %fusion.4, bf16[640,2880]{1,0:T(8,128)(2,1)} %bitcast.12, bf16[1,2880,1440]{1,2,0:T(8,128)(2,1)} %param.10), kind=kOutput, calls=%fused_computation.14 | convolution fusion | flops 5318553600 | bytes 19353600 | tf_op jit(solution)/shard_map/dot_general | solution.py:75
  204.5 11.8 %fusion.8 = bf16[640,2880]{0,1:T(8,128)(2,1)} fusion(bf16[640,1440]{0,1:T(8,128)(2,1)} %get-tuple-element.4, bf16[1,2880,1440]{1,2,0:T(8,128)(2,1)} %param.10), kind=kOutput, calls=%fused_computation.11 | convolution fusion | flops 5310259200 | bytes 13824000 | tf_op jit(solution)/shard_map/dot_general | solution.py:19
  216.3 6.2 %copy.25 = bf16[640,2880]{1,0:T(8,128)(2,1)} copy(bf16[640,2880]{0,1:T(8,128)(2,1)} %fusion.8) | data formatting | bytes 7372800 | tf_op jit(solution)/shard_map/convert_element_type | solution.py:82
  222.4 4.8 %all-to-all-start.2 = ((bf16[16,40,2880]{2,1,0:T(8,128)(2,1)}), bf16[16,40,2880]{2,1,0:T(8,128)(2,1)}, u32[]{:S(2)}, u32[]{:S(2)}) async-start(bf16[16,40,2880]{2,1,0:T(8,128)(2,1)} %bitcast.51), calls=%async_computation.2 | async-start | bytes 7536640 | tf_op jit(solution)/shard_map/all_to_all | solution.py:65
  227.2 6.1 %copy.27 = bf16[640,2880]{0,1:T(8,128)(2,1)} copy(bf16[640,2880]{1,0:T(8,128)(2,1)} %bitcast.9) | data formatting | bytes 7372800 | tf_op jit(solution)/shard_map/all_to_all | solution.py:65
  233.3 1.2 collective-permute-start.3
  234.5 0.3 collective-permute-start.1
  234.8 2.8 broadcast_select_fusion
  237.5 2.3 copy.26
  239.8 1.2 collective-permute-start
  241.0 1.6 broadcast_select_fusion.1
  242.5 0.0 copy-start.3
  242.6 0.3 collective-permute-start.2
  242.9 7.6 %fusion.12 = f32[1440,1440]{1,0:T(8,128)S(1)} fusion(bf16[640,1440]{0,1:T(8,128)(2,1)} %get-tuple-element.4, pred[]{:T(512)S(6)} %eq.96, bf16[640,2880]{1,0:T(8,128)(2,1)} %bitcast.12), kind=kOutput, calls=%fused_computation.18 | convolution fusion | flops 2655129600 | bytes 14069761 | tf_op jit(solution)/shard_map/dot_general | solution.py:13
  250.4 0.0 copy-done.3
  250.4 5.7 %fusion.17 = f32[720,2880]{1,0:T(8,128)S(1)} fusion(bf16[640,2880]{1,0:T(8,128)(2,1)} %bitcast.9, pred[]{:T(512)S(6)} %eq.96, bf16[640,1440]{0,1:T(8,128)(2,1)S(1)} %copy-done.3), kind=kOutput, calls=%fused_computation.25 | convolution fusion | flops 2654668800 | bytes 13824001 | tf_op jit(solution)/shard_map/dot_general | solution.py:13
  256.1 97.8 %collective-permute-done.1 = bf16[640,1440]{0,1:T(8,128)(2,1)} collective-permute-done((bf16[640,1440]{0,1:T(8,128)(2,1)}, bf16[640,1440]{0,1:T(8,128)(2,1)}, u32[]{:S(2)}, u32[]{:S(2)}) %collective-permute-start.1) | collective-permute-done | bytes 1843232 | tf_op jit(solution)/shard_map/ppermute | solution.py:26
  354.0 39.4 %collective-permute-done = bf16[640,1440]{0,1:T(8,128)(2,1)S(1)} collective-permute-done((bf16[640,1440]{0,1:T(8,128)(2,1)}, bf16[640,1440]{0,1:T(8,128)(2,1)S(1)}, u32[]{:S(2)}, u32[]{:S(2)}) %collective-permute-start) | collective-permute-done | bytes 1843232 | tf_op jit(solution)/shard_map/ppermute | solution.py:26
  393.3 6.8 %fusion.7 = bf16[1,1440,1440]{2,1,0:T(8,128)(2,1)} fusion(f32[1440,1440]{1,0:T(8,128)S(1)} %fusion.12, bf16[640,1440]{0,1:T(8,128)(2,1)S(1)} %collective-permute-done, bf16[640,1440]{0,1:T(8,128)(2,1)} %collective-permute-done.1), kind=kOutput, calls=%fused_computation.10 | convolution fusion | flops 2658355200 | bytes 16128000 | tf_op jit(solution)/shard_map/dot_general | solution.py:13
  400.1 13.0 %collective-permute-done.2 = bf16[640,720]{0,1:T(8,128)(2,1)S(1)} collective-permute-done((bf16[640,720]{0,1:T(8,128)(2,1)S(1)}, bf16[640,720]{0,1:T(8,128)(2,1)S(1)}, u32[]{:S(2)}, u32[]{:S(2)}) %collective-permute-start.2) | collective-permute-done | bytes 921632 | tf_op jit(solution)/shard_map/ppermute | solution.py:26
  413.1 0.0 collective-permute-done.3
  413.1 0.0 copy-start.1
  413.1 7.4 %fusion.11 = bf16[1,720,2880]{2,1,0:T(8,128)(2,1)} fusion(f32[720,2880]{1,0:T(8,128)S(1)} %fusion.17, bf16[640,720]{0,1:T(8,128)(2,1)S(1)} %collective-permute-done.2, bf16[640,2880]{0,1:T(8,128)(2,1)} %collective-permute-done.3), kind=kOutput, calls=%fused_computation.13 | convolution fusion | flops 2658355200 | bytes 17049600 | tf_op jit(solution)/shard_map/dot_general | solution.py:13
  420.5 0.0 all-to-all-done.2
  420.5 4.5 %convolution_convert_fusion.1 = bf16[128,2880]{0,1:T(8,128)(2,1)} fusion(bf16[640,2880]{1,0:T(8,128)(2,1)} %bitcast.15, s32[128]{0:T(128)S(1)} %get-tuple-element.6, s32[128]{0:T(128)S(1)} %get-tuple-element.7, s32[128]{0:T(128)S(1)} %get-tuple-element.8, s32[128]{0:T(128)S(1)} %get-tuple-element.5), kind=kOutput, calls=%fused_computation.17 | convolution fusion | flops 472965120 | bytes 4425728 | tf_op jit(solution)/shard_map/dot_general | solution.py:86
  425.0 0.0 copy-done.1
  (1 shorter events, 0.0 us)
Async XLA Ops:
  0.6 3.4 copy-start
  13.3 6.7 %copy-start.2 = (bf16[128,2880]{0,1:T(8,128)(2,1)S(1)}, bf16[128,2880]{0,1:T(8,128)(2,1)}, u32[]{:S(2)}) copy-start(bf16[128,2880]{0,1:T(8,128)(2,1)} %param.6) | copy-start | bytes 2211844
  13.3 90.0 %all-to-all-start = ((bf16[16,40,2880]{2,1,0:T(8,128)(2,1)}), bf16[16,40,2880]{2,1,0:T(8,128)(2,1)}, u32[]{:S(2)}, u32[]{:S(2)}) async-start(bf16[16,40,2880]{2,1,0:T(8,128)(2,1)} %bitcast.53), calls=%async_computation | async-start | bytes 7536640 | tf_op jit(solution)/shard_map/all_to_all | solution.py:65
  103.3 88.1 %all-to-all-start.1 = ((bf16[16,40,2880]{2,1,0:T(8,128)(2,1)}), bf16[16,40,2880]{2,1,0:T(8,128)(2,1)}, u32[]{:S(2)}, u32[]{:S(2)}) async-start(bf16[16,40,2880]{2,1,0:T(8,128)(2,1)} %bitcast.52), calls=%async_computation.1 | async-start | bytes 7536640 | tf_op jit(solution)/shard_map/all_to_all | solution.py:65
  222.4 198.0 %all-to-all-start.2 = ((bf16[16,40,2880]{2,1,0:T(8,128)(2,1)}), bf16[16,40,2880]{2,1,0:T(8,128)(2,1)}, u32[]{:S(2)}, u32[]{:S(2)}) async-start(bf16[16,40,2880]{2,1,0:T(8,128)(2,1)} %bitcast.51), calls=%async_computation.2 | async-start | bytes 7536640 | tf_op jit(solution)/shard_map/all_to_all | solution.py:65
  233.3 179.8 %collective-permute-start.3 = (bf16[640,2880]{0,1:T(8,128)(2,1)}, bf16[640,2880]{0,1:T(8,128)(2,1)}, u32[]{:S(2)}, u32[]{:S(2)}) collective-permute-start(bf16[640,2880]{0,1:T(8,128)(2,1)} %copy.27), channel_id=1, source_target_pairs={{0,16},{16,0},{1,17},{17,1},{2,18},{18,2},{3,19},{19,3},{4,20},{20... | collective-permute-start | bytes 11059208 | tf_op jit(solution)/shard_map/ppermute | solution.py:26
  234.5 119.5 %collective-permute-start.1 = (bf16[640,1440]{0,1:T(8,128)(2,1)}, bf16[640,1440]{0,1:T(8,128)(2,1)}, u32[]{:S(2)}, u32[]{:S(2)}) collective-permute-start(bf16[640,1440]{0,1:T(8,128)(2,1)} %get-tuple-element.4), channel_id=1, source_target_pairs={{0,16},{16,0},{1,17},{17,1},{2,18},{18,2},{3,19},{19,3},{4,20},{20... | collective-permute-start | bytes 5529608 | tf_op jit(solution)/shard_map/ppermute | solution.py:26
  239.8 153.6 %collective-permute-start = (bf16[640,1440]{0,1:T(8,128)(2,1)}, bf16[640,1440]{0,1:T(8,128)(2,1)S(1)}, u32[]{:S(2)}, u32[]{:S(2)}) collective-permute-start(bf16[640,1440]{0,1:T(8,128)(2,1)} %copy.26), channel_id=1, source_target_pairs={{0,16},{16,0},{1,17},{17,1},{2,18},{18,2},{3,19},{19,3},{4,20},{20... | collective-permute-start | bytes 5529608 | tf_op jit(solution)/shard_map/ppermute | solution.py:26
  242.5 7.9 %copy-start.3 = (bf16[640,1440]{0,1:T(8,128)(2,1)S(1)}, bf16[640,1440]{0,1:T(8,128)(2,1)}, u32[]{:S(2)}) copy-start(bf16[640,1440]{0,1:T(8,128)(2,1)} %get-tuple-element.3) | copy-start | bytes 5529604
  242.6 170.5 %collective-permute-start.2 = (bf16[640,720]{0,1:T(8,128)(2,1)S(1)}, bf16[640,720]{0,1:T(8,128)(2,1)S(1)}, u32[]{:S(2)}, u32[]{:S(2)}) collective-permute-start(bf16[640,720]{0,1:T(8,128)(2,1)S(1)} %broadcast_select_fusion.1), channel_id=1, source_target_pairs={{0,16},{16,0},{1,17},{17,1},{2,18},{18,2},{3,19},{19,3},{4,20},{20... | collective-permute-start | bytes 2764808 | tf_op jit(solution)/shard_map/ppermute | solution.py:26
  413.1 11.9 %copy-start.1 = (bf16[128,2880]{0,1:T(8,128)(2,1)S(1)}, bf16[128,2880]{0,1:T(8,128)(2,1)}, u32[]{:S(2)}) copy-start(bf16[128,2880]{0,1:T(8,128)(2,1)} %param.7) | copy-start | bytes 2211844
